TPU v7x, 32 devices: a whole 2x2x4 slice. The times are simulated.
32 devices in a mesh: ab: 4 (over x, core), kl: 4 (over z), ij: 2 (over y).
Axes of the slice: x: 2, y: 2, z: 4, core: 2. Of those that a mesh axis runs over, the one named last changes fastest.
Arguments:
- amplitudes: bfloat16 [2048, 8192], P('ab', ('kl', 'ij')), may hold values from -6 to 6
- integrals: bfloat16 [8192, 8192], P(('kl', 'ab'), 'ij'), may hold values from -0.0625 to 0.0625
Outputs:
- ladder: float32 [2048, 8192], P('ab', ('ij', 'kl'))
All inputs are finite; a program needn't handle non-finite values.
Results may differ from a plain program's by a relative error of at most 0.0003.
Values may be sent and summed in bfloat16 or wider, within the bound.
A program may use at most 64 MiB of HBM per device.

v0:
```python
import jax
import jax.numpy as jnp
from jax import lax
from jax.sharding import PartitionSpec as P

PAIRS = 8128


def per_device(amplitudes, integrals):
    kl_index = lax.axis_index("kl")
    ij_index = lax.axis_index("ij")
    blocked = lax.all_gather(amplitudes, "ij", axis=1, tiled=True)
    col_count = blocked.shape[1]
    col_ids = kl_index * col_count + jnp.arange(col_count)
    masked = jnp.where((col_ids < PAIRS)[None, :], blocked, jnp.zeros((), jnp.bfloat16))
    partial_terms = jnp.dot(
        masked,
        lax.all_gather(integrals, "ab", axis=0, tiled=True),
        preferred_element_type=jnp.float32,
    )
    owned = lax.psum_scatter(partial_terms, "kl", scatter_dimension=1, tiled=True)
    out_width = owned.shape[1]
    out_ids = ij_index * integrals.shape[1] + kl_index * out_width + jnp.arange(out_width)
    return jnp.where((out_ids < PAIRS)[None, :], owned, jnp.float32(0.0))


def solution(mesh):
    in_specs = (P("ab", ("kl", "ij")), P(("kl", "ab"), "ij"))
    out_specs = P("ab", ("ij", "kl"))
    return jax.shard_map(
        per_device, mesh=mesh, in_specs=in_specs, out_specs=out_specs, check_vma=False
    )
```

profile of v0, /device:TPU:26, one launch (start us, length us, event | category | flops | bytes accessed | tf_op | source)
XLA Modules:
  0.0 319.6 jit_solution(1980656232763784469)
XLA Ops:
  6.5 0.0 all-gather.3.cloned.1.call-start
  6.5 0.7 all-gather.3.cloned.1.call-update
  7.3 0.0 all-gather.5.cloned.1.call-start
  7.3 0.7 all-gather.5.cloned.1.call-update
  8.0 0.0 reduce-scatter.2.cloned.1.call-start
  8.1 34.9 %all-gather.3.cloned.1.call-done = bf16[512,2048]{1,0:T(8,128)(2,1)} async-done(((bf16[512,1024]{1,0:T(8,128)(2,1)}), bf16[512,2048]{1,0:T(8,128)(2,1)}) %all-gather.3.cloned.1.call-update) | async-done | bytes 2097168 | tf_op jit(solution)/shard_map/all_gather | solution.py:12
  43.0 106.6 %all-gather.5.cloned.1.call-done = bf16[2048,4096]{1,0:T(8,128)(2,1)} async-done(((bf16[512,4096]{1,0:T(8,128)(2,1)}), bf16[2048,4096]{1,0:T(8,128)(2,1)}) %all-gather.5.cloned.1.call-update) | async-done | bytes 16777232 | tf_op jit(solution)/shard_map/all_gather | solution.py:18
  149.5 15.0 %fusion = f32[512,4096]{1,0:T(8,128)} fusion(bf16[2048,4096]{1,0:T(8,128)(2,1)} %all-gather.5.cloned.1.call-done, bf16[512,2048]{1,0:T(8,128)(2,1)} %all-gather.3.cloned.1.call-done, pred[2048]{0:T(1024)(128)(4,1)S(1)} %add_compare_fusion), kind=kOutput, calls=%fused_computation | convolution fusion | flops 8590983168 | bytes 27265024 | tf_op jit(solution)/shard_map/dot_general | solution.py:16
  164.5 0.0 reduce-scatter.2.cloned.1.call-update
  164.6 145.3 %reduce-scatter.2.cloned.1.call-done = f32[512,1024]{1,0:T(8,128)} async-done(((f32[512,4096]{1,0:T(8,128)}), f32[512,1024]{1,0:T(8,128)}) %reduce-scatter.2.cloned.1.call-update) | async-done | bytes 2097168 | tf_op jit(solution)/shard_map/reduce_scatter | solution.py:21
  309.8 3.2 %broadcast_select_fusion = f32[512,1024]{1,0:T(8,128)} fusion(f32[512,1024]{1,0:T(8,128)} %reduce-scatter.2.cloned.1.call-done, pred[1024]{0:T(1024)(128)(4,1)S(1)} %add_compare_fusion.1), kind=kLoop, calls=%fused_computation.3 | loop fusion | flops 524288 | bytes 4195328 | tf_op jit(solution)/shard_map/jit(_where)/select_n | solution.py:24
  (2 shorter events, 0.0 us)
Async XLA Ops:
  6.5 36.4 %all-gather.3.cloned.1.call-start = ((), (), s32[]{:S(2)}) async-start(), calls=%async_computation.1 | async-start | bytes 3145728 | tf_op jit(solution)/shard_map/all_gather | solution.py:12
  7.3 142.3 %all-gather.5.cloned.1.call-start = ((), (), s32[]{:S(2)}) async-start(), calls=%async_computation.2 | async-start | bytes 20971520 | tf_op jit(solution)/shard_map/all_gather | solution.py:18
  8.0 301.8 %reduce-scatter.2.cloned.1.call-start = ((), (), s32[]{:S(2)}) async-start(), calls=%async_computation.3 | async-start | bytes 10485760 | tf_op jit(solution)/shard_map/reduce_scatter | solution.py:21
Sparse Core Ops, SparseCore 0:
  8.9 34.0 all-gather.2
  44.5 104.9 all-gather.4
  164.7 145.1 reduce-scatter.1
where the time goes:
time: 322 us; the launch traced here: 320 us
  waiting for transfers between devices  288 us (89%)
  matrix products  15 us (5%)
  between operations  13.1 us (4%)
  other arithmetic  3.23 us (1%)
    reduce_scatter x1, waiting for transfers between devices, per_device(): lax.psum_scatter(partial_terms, 'kl', scatter_dimension=1, tiled=True)  145 us
    all_gather x1, waiting for transfers between devices, per_device(): lax.all_gather(integrals, 'ab', axis=0, tiled=True)  107 us
    all_gather x1, waiting for transfers between devices, per_device(): blocked = lax.all_gather(amplitudes, 'ij', axis=1, tiled=True)  34.9 us
    dot_general x1, matrix products, per_device(): jnp.dot(masked, lax.all_gather(integrals, 'ab', axis=0, tiled=True), pref...  15 us
  transfers between devices with their start and end apart: 3, of which 3 were waited for; matrix products, arithmetic and copies ran while one was open for 0% of the time, Pallas kernels for 0%

commit v1 on v0

v1 whole, which is shorter than its diff:
```python
import functools
import math

import jax
import jax.numpy as jnp
from jax import lax
from jax.experimental import pallas as pl
from jax.experimental.pallas import tpu as pltpu
from jax.sharding import PartitionSpec as P

PAIRS = 8128
MESH = pl.DeviceIdType.MESH
CHUNK = 256
TOP = 2.0**7.75
HEAD = 16


def visit_order(n):
    return [sorted(range(n), key=lambda d: (-abs(d - k), d > k)) for k in range(n)]


def encode_into(buf, slot, value):
    peak = jnp.max(jnp.abs(value), axis=0, keepdims=True)
    held = jnp.maximum(peak, 1e-30).astype(jnp.bfloat16)
    scaled = value * (TOP / held.astype(jnp.float32))
    p2 = scaled * scaled
    p4 = p2 * p2
    p8 = p4 * p4
    p16 = p8 * p8
    rows = value.shape[0]
    buf[slot, pl.ds(0, rows), :] = jnp.where(scaled < 0, -p16, p16).astype(jnp.bfloat16)
    buf[slot, pl.ds(rows, HEAD), :] = jnp.broadcast_to(held, (HEAD, held.shape[1]))


def decode(buf, slot, rows):
    code = buf[slot, pl.ds(0, rows), :].astype(jnp.float32)
    held = buf[slot, pl.ds(rows, HEAD), :].astype(jnp.float32)[:1]
    size = jnp.sqrt(jnp.sqrt(jnp.sqrt(jnp.sqrt(jnp.abs(code)))))
    return jnp.where(code < 0, -size, size) * (held * (1.0 / TOP))


def kernel(n_ab, n_kl, n_ij, w, a_ref, b_ref, o_ref, ag, bg, lb, rb, sb, acc,
           a_s, a_r, x_s, x_r, f_s, f_r, c_s, c_r, l_r, z_s, zl_r, zr_r):
    ab, kl, ij = lax.axis_index("ab"), lax.axis_index("kl"), lax.axis_index("ij")
    n_pair = n_ab // 2
    pair, core = ab // 2, ab % 2
    sib = ab + 1 - 2 * core
    m, ka = a_ref.shape
    r = b_ref.shape[0]
    width = o_ref.shape[1]
    per = width // w
    chunks = n_kl * per
    orders = visit_order(n_kl)

    def peer(o):
        return ((pair + o) % n_pair) * 2 + core

    def source(o):
        return ((pair + n_pair - o) % n_pair) * 2 + core

    def dest_of(i):
        t = i // per
        d = jnp.int32(0)
        for k in range(n_kl):
            for u in range(n_kl):
                d = jnp.where((kl == k) & (t == u), orders[k][u], d)
        return d

    def cols_of(i):
        return pl.ds(pl.multiple_of(dest_of(i) * width + (i % per) * w, w), w)

    def rows_of(dev):
        return pl.ds(pl.multiple_of(dev * r, r), r)

    barrier = pltpu.get_barrier_semaphore()

    def greet(dev):
        pl.semaphore_signal(barrier, inc=1, device_id=dev, device_id_type=MESH)

    for o in range(1, n_pair):
        greet((peer(o), kl, ij))
    greet((sib, kl, ij))
    for o in range(1, n_ij):
        greet((ab, kl, (ij + o) % n_ij))

    @pl.when(kl > 0)
    def _():
        greet((ab, kl - 1, ij))

    @pl.when(kl < n_kl - 1)
    def _():
        greet((ab, kl + 1, ij))

    lines = (kl > 0).astype(jnp.int32) + (kl < n_kl - 1).astype(jnp.int32)
    pl.semaphore_wait(barrier, n_pair + n_ij - 1 + lines)

    def a_copy(o):
        return pltpu.make_async_remote_copy(
            a_ref, ag.at[ij], a_s.at[o - 1], a_r.at[o - 1],
            device_id=(ab, kl, (ij + o) % n_ij), device_id_type=MESH)

    def x_copy(i, o):
        return pltpu.make_async_remote_copy(
            b_ref.at[:, cols_of(i)], bg.at[i, rows_of(ab), :],
            x_s.at[i, o - 1], x_r.at[i, o - 1],
            device_id=(peer(o), kl, ij), device_id_type=MESH)

    def f_copy(i, o):
        there = bg.at[i, rows_of(source(o)), :]
        return pltpu.make_async_remote_copy(
            there, there, f_s.at[i, o - 1], f_r.at[i, o - 1],
            device_id=(sib, kl, ij), device_id_type=MESH)

    def c_copy(i):
        return pltpu.make_async_remote_copy(
            b_ref.at[:, cols_of(i)], bg.at[i, rows_of(ab), :], c_s.at[i], c_r.at[i],
            device_id=(sib, kl, ij), device_id_type=MESH)

    def l_copy(i):
        return pltpu.make_async_copy(
            b_ref.at[:, cols_of(i)], bg.at[i, rows_of(ab), :], l_r.at[i])

    def z_copy(i, slot, up):
        box, sem = (lb, zl_r) if up else (rb, zr_r)
        return pltpu.make_async_remote_copy(
            sb.at[i], box.at[slot], z_s.at[i], sem.at[slot],
            device_id=(ab, kl + 1 if up else kl - 1, ij), device_id_type=MESH)

    for o in range(1, n_ij):
        a_copy(o).start()

    def begin(i, carry):
        for o in range(1, n_pair):
            x_copy(i, o).start()
        c_copy(i).start()
        l_copy(i).start()
        return carry

    lax.fori_loop(0, chunks, begin, 0)

    ag[ij] = a_ref[...]
    for o in range(1, n_ij):
        a_copy(o).wait_recv()
    for j in range(n_ij):
        first = kl * (ka * n_ij) + j * ka

        @pl.when(first + ka > PAIRS)
        def _():
            ids = first + lax.broadcasted_iota(jnp.int32, (m, ka), 1)
            ag[j] = jnp.where(ids < PAIRS, ag[j].astype(jnp.float32), 0.0).astype(jnp.bfloat16)

    def step(i, carry):
        for o in range(1, n_pair):
            x_copy(i, o).wait_recv()
            f_copy(i, o).start()
        l_copy(i).wait()
        c_copy(i).wait_recv()
        for o in range(1, n_pair):
            f_copy(i, o).wait_recv()
        total = jnp.dot(ag[0], bg[i, pl.ds(0, ka), :], preferred_element_type=jnp.float32)
        for j in range(1, n_ij):
            total += jnp.dot(ag[j], bg[i, pl.ds(j * ka, ka), :], preferred_element_type=jnp.float32)
        acc[...] = total
        d = dest_of(i)
        slot = d * per + i % per

        @pl.when((d >= kl) & (kl > 0))
        def _():
            z_copy(i, slot, True).wait_recv()
            acc[...] += decode(lb, slot, m)

        @pl.when((d <= kl) & (kl < n_kl - 1))
        def _():
            z_copy(i, slot, False).wait_recv()
            acc[...] += decode(rb, slot, m)

        @pl.when(d == kl)
        def _():
            first = pl.multiple_of((i % per) * w, w)
            ids = (ij * n_kl + kl) * width + first + lax.broadcasted_iota(jnp.int32, (m, w), 1)
            o_ref[:, pl.ds(first, w)] = jnp.where(ids < PAIRS, acc[...], 0.0)

        @pl.when(d != kl)
        def _():
            encode_into(sb, i, acc[...])

        @pl.when(d > kl)
        def _():
            z_copy(i, slot, True).start()

        @pl.when(d < kl)
        def _():
            z_copy(i, slot, False).start()

        return carry

    lax.fori_loop(0, chunks, step, 0)

    for o in range(1, n_ij):
        a_copy(o).wait_send()

    def drain(i, carry):
        for o in range(1, n_pair):
            x_copy(i, o).wait_send()
            f_copy(i, o).wait_send()
        c_copy(i).wait_send()

        @pl.when(dest_of(i) > kl)
        def _():
            z_copy(i, 0, True).wait_send()

        @pl.when(dest_of(i) < kl)
        def _():
            z_copy(i, 0, False).wait_send()

        return carry

    lax.fori_loop(0, chunks, drain, 0)


def per_device(n_ab, n_kl, n_ij, amplitudes, integrals):
    m, ka = amplitudes.shape
    r, n = integrals.shape
    width = n // n_kl
    w = math.gcd(CHUNK, width)
    chunks = n // w
    others = max(n_ab // 2 - 1, 1)
    mail = pltpu.VMEM((chunks, m + HEAD, w), jnp.bfloat16)
    dma = pltpu.SemaphoreType.DMA
    return pl.pallas_call(
        functools.partial(kernel, n_ab, n_kl, n_ij, w),
        out_shape=jax.ShapeDtypeStruct((m, width), jnp.float32),
        in_specs=[pl.BlockSpec(memory_space=pltpu.VMEM), pl.BlockSpec(memory_space=pl.ANY)],
        out_specs=pl.BlockSpec(memory_space=pltpu.VMEM),
        scratch_shapes=[
            pltpu.VMEM((n_ij, m, ka), jnp.bfloat16),
            pltpu.VMEM((chunks, n_ab * r, w), jnp.bfloat16),
            mail, mail, mail,
            pltpu.VMEM((m, w), jnp.float32),
            dma((max(n_ij - 1, 1),)), dma((max(n_ij - 1, 1),)),
            dma((chunks, others)), dma((chunks, others)),
            dma((chunks, others)), dma((chunks, others)),
            dma((chunks,)), dma((chunks,)), dma((chunks,)),
            dma((chunks,)), dma((chunks,)), dma((chunks,)),
        ],
        compiler_params=pltpu.CompilerParams(
            collective_id=0, has_side_effects=True, vmem_limit_bytes=56 * 2**20),
    )(amplitudes, integrals)


def solution(mesh):
    sizes = [mesh.shape[name] for name in ("ab", "kl", "ij")]
    in_specs = (P("ab", ("kl", "ij")), P(("kl", "ab"), "ij"))
    out_specs = P("ab", ("ij", "kl"))
    return jax.shard_map(
        functools.partial(per_device, *sizes), mesh=mesh, in_specs=in_specs,
        out_specs=out_specs, check_vma=False
    )
```

time: 322 us -> 113 us (0.35)
  waiting for transfers between devices: 288 us -> 0 us
  Pallas kernels: 0 us -> 110 us
  matrix products: 15 us -> 0 us
  between operations: 13.1 us -> 0.01 us
  other arithmetic: 3.23 us -> 0 us
    reduce_scatter x1 -> x0, waiting for transfers between devices: 145 us -> none  [per_device(): lax.psum_scatter(partial_terms, 'kl', scatter_dimension=1, tiled=True)]
    all_gather x2 -> x0, waiting for transfers between devices: 141 us -> none  [the longest x1 107 us: per_device(): lax.all_gather(integrals, 'ab', axis=0, tiled=True)]
    pallas_call x0 -> x1, Pallas kernels: none -> 110 us  [per_device(): pl.pallas_call(functools.partial(kernel, n_ab, n_kl, n_ij, w), out_shape=...]
    dot_general x1 -> x0, matrix products: 15 us -> none  [per_device(): jnp.dot(masked, lax.all_gather(integrals, 'ab', axis=0, tiled=True), pref...]
  transfers between devices with their start and end apart: 3 -> 0, of which waited for: 3 -> 0; matrix products, arithmetic and copies ran while one was open for 0% -> 0% of each run, Pallas kernels for 0% -> 0%
where the time goes in v1:
time: 113 us
  Pallas kernels  110 us (97%)
  local copies, waits for them, and re-layouts  3.16 us (3%)
    pallas_call x1, Pallas kernels, per_device(): pl.pallas_call(functools.partial(kernel, n_ab, n_kl, n_ij, w), out_shape=...  110 us
    unnamed x1, local copies, waits for them, and re-layouts  3.16 us

profile of v1, /device:TPU:26, one launch (start us, length us, event | category | flops | bytes accessed | tf_op | source)
XLA Modules:
  0.0 112.8 jit_solution(1265761932292592966)
XLA Ops:
  0.0 109.6 %shard_map.28 = f32[512,1024]{1,0:T(8,128)} custom-call(bf16[512,1024]{1,0:T(8,128)(2,1)} %a_ref.1, bf16[512,4096]{1,0:T(8,128)(2,1)} %b_ref.1), custom_call_target="tpu_custom_call" | custom-call | tf_op jit(solution)/shard_map/pallas_call | solution.py:230
  109.6 3.2 %copy.4 = f32[512,1024]{1,0:T(8,128)} copy(f32[512,1024]{1,0:T(8,128)} %shard_map.28) | data formatting | bytes 4194304

commit v2 on v1

v2 whole, which is shorter than its diff:
```python
import functools
import math

import jax
import jax.numpy as jnp
from jax import lax
from jax.experimental import pallas as pl
from jax.experimental.pallas import tpu as pltpu
from jax.sharding import PartitionSpec as P

PAIRS = 8128
MESH = pl.DeviceIdType.MESH
CHUNK = 256
TOP = 2.0**7.75
HEAD = 16
PIECES = 2


def visit_order(n):
    return [sorted(range(n), key=lambda d: (-abs(d - k), d > k)) for k in range(n)]


def encode_into(buf, slot, q, value):
    peak = jnp.max(jnp.abs(value), axis=0, keepdims=True)
    held = jnp.maximum(peak, 1e-30).astype(jnp.bfloat16)
    scaled = value * (TOP / held.astype(jnp.float32))
    p2 = scaled * scaled
    p4 = p2 * p2
    p8 = p4 * p4
    p16 = p8 * p8
    rows = value.shape[0]
    buf[slot, q, pl.ds(0, rows), :] = jnp.where(scaled < 0, -p16, p16).astype(jnp.bfloat16)
    buf[slot, q, pl.ds(rows, HEAD), :] = jnp.broadcast_to(held, (HEAD, held.shape[1]))


def decode(buf, slot, q, rows):
    code = buf[slot, q, pl.ds(0, rows), :].astype(jnp.float32)
    held = buf[slot, q, pl.ds(rows, HEAD), :].astype(jnp.float32)[:1]
    size = jnp.sqrt(jnp.sqrt(jnp.sqrt(jnp.sqrt(jnp.abs(code)))))
    return jnp.where(code < 0, -size, size) * (held * (1.0 / TOP))


def kernel(n_ab, n_kl, n_ij, w, pieces, a_ref, b_ref, o_ref, ag, bg, lb, rb, sb, acc,
           a_s, a_r, x_s, x_r, f_s, f_r, c_s, c_r, l_r, z_s, zl_r, zr_r):
    ab, kl, ij = lax.axis_index("ab"), lax.axis_index("kl"), lax.axis_index("ij")
    n_pair = n_ab // 2
    pair, core = ab // 2, ab % 2
    sib = ab + 1 - 2 * core
    m, ka = a_ref.shape
    r = b_ref.shape[0]
    width = o_ref.shape[1]
    per = width // w
    chunks = n_kl * per
    orders = visit_order(n_kl)
    mp = m // pieces
    lead = min(pieces, chunks)

    def peer(o):
        return ((pair + o) % n_pair) * 2 + core

    def source(o):
        return ((pair + n_pair - o) % n_pair) * 2 + core

    def dest_of(i):
        t = i // per
        d = jnp.int32(0)
        for k in range(n_kl):
            for u in range(n_kl):
                d = jnp.where((kl == k) & (t == u), orders[k][u], d)
        return d

    def cols_of(i):
        return pl.ds(pl.multiple_of(dest_of(i) * width + (i % per) * w, w), w)

    def rows_of(dev):
        return pl.ds(pl.multiple_of(dev * r, r), r)

    barrier = pltpu.get_barrier_semaphore()

    def greet(dev):
        pl.semaphore_signal(barrier, inc=1, device_id=dev, device_id_type=MESH)

    for o in range(1, n_pair):
        greet((peer(o), kl, ij))
    greet((sib, kl, ij))
    for o in range(1, n_ij):
        greet((ab, kl, (ij + o) % n_ij))

    @pl.when(kl > 0)
    def _():
        greet((ab, kl - 1, ij))

    @pl.when(kl < n_kl - 1)
    def _():
        greet((ab, kl + 1, ij))

    lines = (kl > 0).astype(jnp.int32) + (kl < n_kl - 1).astype(jnp.int32)
    pl.semaphore_wait(barrier, n_pair + n_ij - 1 + lines)

    def slab(q):
        return pl.ds(pl.multiple_of(q * mp, mp), mp)

    def a_copy(o, q):
        return pltpu.make_async_remote_copy(
            a_ref.at[slab(q), :], ag.at[ij, slab(q), :], a_s.at[o - 1, q], a_r.at[o - 1, q],
            device_id=(ab, kl, (ij + o) % n_ij), device_id_type=MESH)

    def x_copy(i, o):
        return pltpu.make_async_remote_copy(
            b_ref.at[:, cols_of(i)], bg.at[i, rows_of(ab), :],
            x_s.at[i, o - 1], x_r.at[i, o - 1],
            device_id=(peer(o), kl, ij), device_id_type=MESH)

    def f_copy(i, o):
        there = bg.at[i, rows_of(source(o)), :]
        return pltpu.make_async_remote_copy(
            there, there, f_s.at[i, o - 1], f_r.at[i, o - 1],
            device_id=(sib, kl, ij), device_id_type=MESH)

    def c_copy(i):
        return pltpu.make_async_remote_copy(
            b_ref.at[:, cols_of(i)], bg.at[i, rows_of(ab), :], c_s.at[i], c_r.at[i],
            device_id=(sib, kl, ij), device_id_type=MESH)

    def l_copy(i):
        return pltpu.make_async_copy(
            b_ref.at[:, cols_of(i)], bg.at[i, rows_of(ab), :], l_r.at[i])

    def z_copy(i, q, slot, up):
        box, sem = (lb, zl_r) if up else (rb, zr_r)
        return pltpu.make_async_remote_copy(
            sb.at[i, q], box.at[slot, q], z_s.at[i, q], sem.at[slot, q],
            device_id=(ab, kl + 1 if up else kl - 1, ij), device_id_type=MESH)

    for q in range(pieces):
        for o in range(1, n_ij):
            a_copy(o, q).start()

    def begin(i, carry):
        for o in range(1, n_pair):
            x_copy(i, o).start()
        c_copy(i).start()
        l_copy(i).start()
        return carry

    lax.fori_loop(0, chunks, begin, 0)

    def take_chunk(i):
        for o in range(1, n_pair):
            x_copy(i, o).wait_recv()
            f_copy(i, o).start()
        l_copy(i).wait()
        c_copy(i).wait_recv()
        for o in range(1, n_pair):
            f_copy(i, o).wait_recv()

    def take_piece(q):
        ag[ij, slab(q), :] = a_ref[slab(q), :]
        for o in range(1, n_ij):
            a_copy(o, q).wait_recv()
        for j in range(n_ij):
            first = kl * (ka * n_ij) + j * ka

            @pl.when(first + ka > PAIRS)
            def _():
                ids = first + lax.broadcasted_iota(jnp.int32, (mp, ka), 1)
                held = ag[j, slab(q), :].astype(jnp.float32)
                ag[j, slab(q), :] = jnp.where(ids < PAIRS, held, 0.0).astype(jnp.bfloat16)

    def unit(u):
        v = jnp.int32(0)
        for k in range(1, lead):
            v += (u >= k * k).astype(jnp.int32)
        left = u - v * v
        own = left <= v
        rest = u - lead * lead
        early = u < lead * lead
        i = jnp.where(early, jnp.where(own, v, left - v - 1), lead + rest // pieces)
        q = jnp.where(early, jnp.where(own, left, v), rest % pieces)
        return i, q

    def step(u, carry):
        i, q = unit(u)

        @pl.when(q == 0)
        def _():
            take_chunk(i)

        @pl.when(i == q)
        def _():
            take_piece(q)

        acc[...] = sum(
            jnp.dot(ag[j, slab(q), :], bg[i, pl.ds(j * ka, ka), :],
                    preferred_element_type=jnp.float32)
            for j in range(n_ij))
        d = dest_of(i)
        slot = d * per + i % per

        @pl.when((d >= kl) & (kl > 0))
        def _():
            z_copy(i, q, slot, True).wait_recv()
            acc[...] += decode(lb, slot, q, mp)

        @pl.when((d <= kl) & (kl < n_kl - 1))
        def _():
            z_copy(i, q, slot, False).wait_recv()
            acc[...] += decode(rb, slot, q, mp)

        @pl.when(d == kl)
        def _():
            first = pl.multiple_of((i % per) * w, w)
            ids = (ij * n_kl + kl) * width + first + lax.broadcasted_iota(jnp.int32, (mp, w), 1)
            o_ref[slab(q), pl.ds(first, w)] = jnp.where(ids < PAIRS, acc[...], 0.0)

        @pl.when(d != kl)
        def _():
            encode_into(sb, i, q, acc[...])

        @pl.when(d > kl)
        def _():
            z_copy(i, q, slot, True).start()

        @pl.when(d < kl)
        def _():
            z_copy(i, q, slot, False).start()

        return carry

    lax.fori_loop(0, chunks * pieces, step, 0)

    for q in range(pieces):
        for o in range(1, n_ij):
            a_copy(o, q).wait_send()

    def drain(i, carry):
        for o in range(1, n_pair):
            x_copy(i, o).wait_send()
            f_copy(i, o).wait_send()
        c_copy(i).wait_send()
        for q in range(pieces):
            @pl.when(dest_of(i) > kl)
            def _():
                z_copy(i, q, 0, True).wait_send()

            @pl.when(dest_of(i) < kl)
            def _():
                z_copy(i, q, 0, False).wait_send()

        return carry

    lax.fori_loop(0, chunks, drain, 0)


def per_device(n_ab, n_kl, n_ij, amplitudes, integrals):
    m, ka = amplitudes.shape
    r, n = integrals.shape
    width = n // n_kl
    w = math.gcd(CHUNK, width)
    chunks = n // w
    others = max(n_ab // 2 - 1, 1)
    pieces = min(PIECES, chunks, m // 16)
    mail = pltpu.VMEM((chunks, pieces, m // pieces + HEAD, w), jnp.bfloat16)
    dma = pltpu.SemaphoreType.DMA
    return pl.pallas_call(
        functools.partial(kernel, n_ab, n_kl, n_ij, w, pieces),
        out_shape=jax.ShapeDtypeStruct((m, width), jnp.float32),
        in_specs=[pl.BlockSpec(memory_space=pltpu.VMEM), pl.BlockSpec(memory_space=pl.ANY)],
        out_specs=pl.BlockSpec(memory_space=pltpu.VMEM),
        scratch_shapes=[
            pltpu.VMEM((n_ij, m, ka), jnp.bfloat16),
            pltpu.VMEM((chunks, n_ab * r, w), jnp.bfloat16),
            mail, mail, mail,
            pltpu.VMEM((m // pieces, w), jnp.float32),
            dma((max(n_ij - 1, 1), pieces)), dma((max(n_ij - 1, 1), pieces)),
            dma((chunks, others)), dma((chunks, others)),
            dma((chunks, others)), dma((chunks, others)),
            dma((chunks,)), dma((chunks,)), dma((chunks,)),
            dma((chunks, pieces)), dma((chunks, pieces)), dma((chunks, pieces)),
        ],
        compiler_params=pltpu.CompilerParams(
            collective_id=0, has_side_effects=True, vmem_limit_bytes=56 * 2**20),
    )(amplitudes, integrals)


def solution(mesh):
    sizes = [mesh.shape[name] for name in ("ab", "kl", "ij")]
    in_specs = (P("ab", ("kl", "ij")), P(("kl", "ab"), "ij"))
    out_specs = P("ab", ("ij", "kl"))
    return jax.shard_map(
        functools.partial(per_device, *sizes), mesh=mesh, in_specs=in_specs,
        out_specs=out_specs, check_vma=False
    )
```

time: 113 us -> 107 us (0.947)
  Pallas kernels: 110 us -> 103 us
    pallas_call x1, Pallas kernels: 110 us -> 103 us  [per_device(): pl.pallas_call(functools.partial(kernel, n_ab, n_kl, n_ij, w, pieces), ou...]
where the time goes in v2:
time: 107 us; the launch traced here: 106 us
  Pallas kernels  103 us (96%)
  local copies, waits for them, and re-layouts  3.16 us (3%)
    pallas_call x1, Pallas kernels, per_device(): pl.pallas_call(functools.partial(kernel, n_ab, n_kl, n_ij, w, pieces), ou...  103 us
    unnamed x1, local copies, waits for them, and re-layouts  3.16 us

profile of v2, /device:TPU:26, one launch (start us, length us, event | category | flops | bytes accessed | tf_op | source)
XLA Modules:
  0.0 105.8 jit_solution(10200794075529053409)
XLA Ops:
  0.0 102.7 %shard_map.28 = f32[512,1024]{1,0:T(8,128)} custom-call(bf16[512,1024]{1,0:T(8,128)(2,1)} %a_ref.1, bf16[512,4096]{1,0:T(8,128)(2,1)} %b_ref.1), custom_call_target="tpu_custom_call" | custom-call | tf_op jit(solution)/shard_map/pallas_call | solution.py:265
  102.7 3.2 %copy.4 = f32[512,1024]{1,0:T(8,128)} copy(f32[512,1024]{1,0:T(8,128)} %shard_map.28) | data formatting | bytes 4194304
